TPU v7x, 32 devices: a whole 2x2x4 slice. The times are simulated.
32 devices in a mesh: pipe: 2 (over core), dp: 8 (over z, y), mp: 2 (over x).
Axes of the slice: x: 2, y: 2, z: 4, core: 2. Of those that a mesh axis runs over, the one named last changes fastest.
Arguments:
- token_ids: int32 [2, 4096], P('pipe', 'dp'), may hold values from 0 to 32127, as said below
- embedded: bfloat16 [2, 4096, 4096], P('pipe', 'dp', 'mp'), may hold values from -720 to 720
- norm_gain: float32 [2, 4096], P('pipe', 'mp'), may hold values from 0.25 to 1.75
- proj_grad: bfloat16 [2, 4096, 2048], P('pipe', 'dp'), may hold values from -6 to 6
- proj_weight: bfloat16 [2, 4096, 2048], P('pipe', 'mp'), may hold values from -0.125 to 0.125
- stream_grad: bfloat16 [2, 4096, 4096], P('pipe', 'dp', 'mp'), may hold values from -6 to 6
Outputs:
- table_grad: float32 [32128, 2, 2048], P('dp', 'mp', 'pipe')
Inputs may be any that keep to these rules, and one draw needn't show every extreme that they name: `token_ids`: call block o the ids o * 4016 to (o + 1) * 4016 - 1. The 512 tokens of one stack on one index of dp hold at most 128 ids of any one block, and some block gets exactly 128 of them.
All inputs are finite; a program needn't handle non-finite values.
Results may differ from a plain program's by a relative error of at most 0.0029.
Values may be sent and summed in bfloat16 or wider, within the bound.
A program may use at most 128 MiB of HBM per device.

v0:
```python
import functools

import jax
import jax.numpy as jnp
from jax import lax
from jax.experimental import pallas as pl
from jax.experimental.pallas import tpu as pltpu
from jax.sharding import PartitionSpec as P

VOCAB = 32128
LANES = 128
epsilon = 1e-06
VMEM_LIMIT = 60 * 1024 * 1024


def partner(me, k, n):
    out, bit = 0, 1
    while bit < n:
        mine = (me // bit) % 2
        flip = (k // bit) % 2
        out = out + bit * (mine + flip - 2 * mine * flip)
        bit *= 2
    return out


def contract_last(a, b):
    return lax.dot_general(a, b, (((1,), (1,)), ((), ())), preferred_element_type=jnp.float32)


def greet_all(n, pipe, other, me, mp):
    barrier = pltpu.get_barrier_semaphore()

    def greet(k, carry):
        d = partner(me, k, n)
        pl.semaphore_signal(
            barrier, inc=1, device_id={"dp": d, "pipe": other}, device_id_type=pl.DeviceIdType.MESH
        )

        @pl.when(k > 0)
        def _():
            pl.semaphore_signal(
                barrier, inc=1, device_id={"dp": d, "pipe": pipe}, device_id_type=pl.DeviceIdType.MESH
            )

        return carry

    lax.fori_loop(0, n, greet, 0)
    if mp is not None:
        pl.semaphore_signal(
            barrier, inc=1, device_id={"mp": 1 - mp}, device_id_type=pl.DeviceIdType.MESH
        )
    return barrier


def find_places(n, keep, spill, block_rows, me, ids_ref, placer_v, local_v, state_v):
    tokens = ids_ref.shape[1]
    ids = ids_ref[...]
    owner = lax.broadcasted_iota(jnp.int32, (n, tokens), 0)
    owner_low = owner * block_rows
    match = (ids >= owner_low) & (ids < owner_low + block_rows)
    match_f = match.astype(jnp.float32)
    before = (
        lax.broadcasted_iota(jnp.int32, (tokens, tokens), 0)
        < lax.broadcasted_iota(jnp.int32, (tokens, tokens), 1)
    ).astype(jnp.float32).astype(jnp.bfloat16)
    rank = match_f * jnp.dot(match_f.astype(jnp.bfloat16), before, preferred_element_type=jnp.float32)
    rank = jnp.sum(rank, axis=0, keepdims=True).astype(jnp.int32)
    token_owner = jnp.sum(jnp.where(match, owner, 0), axis=0, keepdims=True)
    position = jnp.where(rank < keep, partner(me, token_owner, n) * keep + rank, -1)
    local = ids - token_owner * block_rows
    high = local // 64
    row = lax.broadcasted_iota(jnp.int32, (8, tokens), 0)
    parts = jnp.where(row == 0, high, jnp.where(row == 1, local - high * 64, 0))
    parts = jnp.where(row == 2, token_owner + 1, parts)
    local_v[...] = parts.astype(jnp.float32).astype(jnp.bfloat16)
    if spill:
        over = match_f * (rank >= keep).astype(jnp.float32)
        count = jnp.sum(over, axis=1, keepdims=True)
        start = jnp.zeros((1, 1), jnp.float32)
        begin = jnp.zeros((1, tokens), jnp.float32)
        for o in range(n):
            begin = begin + over[o:o + 1] * start
            start = start + count[o:o + 1]
        behind = n * keep + begin.astype(jnp.int32) + rank - keep
        position = jnp.where(rank >= keep, behind, position)
        full = (start > spill).astype(jnp.float32)
        state_v[1:2, :] = jnp.broadcast_to(full, (1, LANES)).astype(jnp.int32)
    slots = lax.broadcasted_iota(jnp.int32, placer_v.shape, 0)
    placer_v[...] = (position == slots).astype(jnp.float32).astype(jnp.bfloat16)


def place_indices(n, keep, spill, me, placer_v, local_v, state_v, sendi_v):
    parts = contract_last(local_v[...], placer_v[...])
    found = (parts[0:1] * 64.0 + parts[1:2]).astype(jnp.int32)
    if spill:
        state_v[0:1, :] = found[:, n * keep:]
        state_v[2:3, :] = parts[2:3, n * keep:].astype(jnp.int32)
        lane = lax.broadcasted_iota(jnp.int32, (1, LANES), 1)
        sendi_v[...] = jnp.zeros(sendi_v.shape, jnp.int32)
    for k in range(n):
        sendi_v[k, :, 0:keep] = found[:, k * keep:(k + 1) * keep]
        if spill:
            d = partner(me, k, n)
            there = state_v[2:3, :]
            count = jnp.sum(((there == d + 1) & (lane < spill)).astype(jnp.float32), axis=1, keepdims=True)
            start = jnp.sum(((there > 0) & (there < d + 1)).astype(jnp.float32), axis=1, keepdims=True)
            facts = jnp.where(lane == 1, count, start).astype(jnp.int32)
            sendi_v[k, :, LANES:2 * LANES] = state_v[0:1, :]
            sendi_v[k, :, 2 * LANES:] = jnp.where(lane == 0, state_v[1:2, :], facts)


def place_rows(c, chunk, keep, spill, placer_v, part, send_v, over_v):
    n, _, _, half = send_v.shape
    p, cols = c * chunk // half, pl.ds(c * chunk % half, chunk)
    placed = jnp.dot(
        placer_v[0:n * keep + spill, :], part, preferred_element_type=jnp.float32
    ).astype(jnp.bfloat16)
    send_v[:, p, :, cols] = placed[:n * keep].reshape(n, keep, chunk)
    if spill:
        over_v[p, :, cols] = placed[n * keep:]


def remote(src, dst, send_sem, recv_sem, **where):
    return pltpu.make_async_remote_copy(
        src_ref=src, dst_ref=dst, send_sem=send_sem, recv_sem=recv_sem,
        device_id=where, device_id_type=pl.DeviceIdType.MESH,
    )


def make_sender(n, pipe, other, me, send_v, sendi_v, rows_out, index_out, sems):
    send_sem, recv_sem, isend_sem, irecv_sem = sems

    def copies(k, p, s):
        d = partner(me, k, n)
        return (
            remote(send_v.at[k, p], rows_out.at[k, s], send_sem.at[k, p], recv_sem.at[k, s], dp=d, pipe=p),
            remote(sendi_v.at[k], index_out.at[k, s], isend_sem.at[k, p], irecv_sem.at[k, s], dp=d, pipe=p),
        )

    def send(k, own_chip):
        for copy in copies(k, other, pipe):
            copy.start()
        if not own_chip:
            for copy in copies(k, pipe, pipe):
                copy.start()

    def arrive(k, carry):
        for copy in copies(k, other, pipe):
            copy.wait_send()
        for copy in copies(k, other, other):
            copy.wait_recv()

        @pl.when(k > 0)
        def _():
            for copy in copies(k, pipe, pipe):
                copy.wait_send()
            for copy in copies(k, other, pipe):
                copy.wait_recv()

        return carry

    return send, arrive


def exchange_kernel(
    n, cap, keep, spill, block_rows, full_width, chunk,
    ids_ref, gain_ref, embedded, proj_grad, weight, stream,
    rows_out, index_out, spill_out, kept_out,
    emb_v, grad_v, weight_v, stream_v, scaled_v, rows_v, send_v, sendi_v, over_v, sums_v, sums_got,
    placer_v, local_v, state_v,
    in_sem, weight_sem, sum_send, sum_recv, send_sem, recv_sem, isend_sem, irecv_sem, own_sem,
    pair_send, pair_recv, line_send, line_recv, side_send, side_recv,
):
    pipe = lax.axis_index("pipe")
    me = lax.axis_index("dp")
    mp = lax.axis_index("mp")
    other = 1 - pipe
    tokens, width = emb_v.shape
    half = width // 2

    loads = [
        pltpu.make_async_copy(proj_grad, grad_v, in_sem.at[0]),
        pltpu.make_async_copy(embedded, emb_v, in_sem.at[1]),
        pltpu.make_async_copy(stream, stream_v, in_sem.at[2]),
    ]
    chunks = [
        pltpu.make_async_copy(
            weight.at[pl.ds(j * chunk, chunk)], weight_v.at[pl.ds(j * chunk, chunk)], weight_sem.at[j]
        )
        for j in range(width // chunk)
    ]
    loads[0].start()
    chunks[0].start()
    loads[1].start()
    for copy in chunks[1:]:
        copy.start()
    loads[2].start()
    barrier = greet_all(n, pipe, other, me, mp)
    find_places(n, keep, spill, block_rows, me, ids_ref, placer_v, local_v, state_v)

    loads[0].wait()
    mixed = jnp.zeros((tokens, 1), jnp.float32)
    square = jnp.zeros((tokens, 1), jnp.float32)
    for j in range(width // chunk):
        cols = pl.ds(j * chunk, chunk)
        chunks[j].wait()
        if j == 0:
            loads[1].wait()
        scaled = contract_last(grad_v[...], weight_v[cols, :]) * gain_ref[:, cols]
        scaled_v[:, cols] = scaled
        inputs = emb_v[:, cols].astype(jnp.float32)
        square = square + jnp.sum(inputs * inputs, axis=1, keepdims=True)
        mixed = mixed + jnp.sum(inputs * scaled, axis=1, keepdims=True)
    lane = lax.broadcasted_iota(jnp.int32, (tokens, LANES), 1)
    packed = jnp.where(lane == 0, square, jnp.where(lane == 1, mixed, 0.0))
    sums_v[...] = packed.T[:8]

    pl.semaphore_wait(barrier, 2 * n)
    swap = remote(sums_v, sums_got, sum_send, sum_recv, mp=1 - mp)
    swap.start()
    place_indices(n, keep, spill, me, placer_v, local_v, state_v, sendi_v)
    loads[2].wait()
    swap.wait()

    total = sums_v[...] + sums_got[...]
    inverse = lax.rsqrt(total[0:1] / full_width + epsilon)
    coef = inverse * inverse * inverse * total[1:2] / full_width
    line = lax.broadcasted_iota(jnp.int32, (LANES, tokens), 0)
    back = jnp.where(line == 0, inverse, jnp.where(line == 1, coef, 0.0)).T
    for j in range(width // chunk):
        cols = pl.ds(j * chunk, chunk)
        norm_back = back[:, 0:1] * scaled_v[:, cols] - emb_v[:, cols].astype(jnp.float32) * back[:, 1:2]
        part = (stream_v[:, cols].astype(jnp.float32) + norm_back).astype(jnp.bfloat16)
        if spill:
            rows_v[:, cols] = part
        place_rows(j, chunk, keep, spill, placer_v, part, send_v, over_v)

    send, arrive = make_sender(
        n, pipe, other, me, send_v, sendi_v, rows_out, index_out,
        (send_sem, recv_sem, isend_sem, irecv_sem),
    )
    if spill:
        lines = n // 2
        at, beside = me // 2, partner(me, 1, n)
        pair = remote(over_v.at[other], spill_out.at[0, pipe], pair_send, pair_recv, pipe=other)
        pair.start()
        own_over = pltpu.make_async_copy(over_v.at[pipe], spill_out.at[0, pipe], own_sem.at[2])
        own_over.start()
        kept = pltpu.make_async_copy(rows_v, kept_out, own_sem.at[3])
        kept.start()

        def along(up, r, source, to):
            return remote(
                spill_out.at[partner(me, source, n)], spill_out.at[partner(to, source, n)],
                line_send.at[up, r], line_recv.at[up, r], dp=to,
            )

        def across(source):
            return remote(
                spill_out.at[partner(me, source, n)], spill_out.at[partner(beside, source, n)],
                side_send.at[source // 2], side_recv.at[source // 2], dp=beside,
            )

        def pass_on(r):
            for up in (1, 0):
                step = 2 if up else -2
                source = me - step * r
                here = (at >= r) if up else (at + r < lines)
                more = (at + 1 < lines) if up else (at >= 1)
                if r > 0:

                    @pl.when(here)
                    def _():
                        remote(
                            spill_out.at[0], spill_out.at[partner(me, source, n)],
                            line_send.at[up, r], line_recv.at[up, r], dp=beside,
                        ).wait_recv()
                        across(source).start()

                @pl.when(here & more)
                def _():
                    along(up, r + 1, source, me + step).start()

            if r == 0:
                across(me).start()

        def finish(r):
            for up in (1, 0):
                step = 2 if up else -2
                source = me - step * r
                here = (at >= r) if up else (at + r < lines)
                more = (at + 1 < lines) if up else (at >= 1)

                @pl.when(here & more)
                def _():
                    along(up, r + 1, source, me + step).wait_send()

        send(1, False)
        own_over.wait()
        pair.wait()
        pass_on(0)
        for k in range(2, n):
            send(k, False)
            if k % 2 == 1 and k // 2 < lines:
                pass_on(k // 2)
        send(0, True)
    else:

        def send_on(k, carry):
            send(k, False)
            return carry

        lax.fori_loop(1, n, send_on, 0)
        send(0, True)
    own_rows = pltpu.make_async_copy(send_v.at[0, pipe], rows_out.at[0, pipe], own_sem.at[0])
    own_index = pltpu.make_async_copy(sendi_v.at[0], index_out.at[0, pipe], own_sem.at[1])
    own_rows.start()
    own_index.start()
    lax.fori_loop(0, n, arrive, 0)
    own_rows.wait()
    own_index.wait()
    if spill:
        for r in range(lines):
            finish(r)

        def side(z, carry):
            remote(
                spill_out.at[partner(me, 2 * z, n)], spill_out.at[partner(me, 2 * z + beside % 2, n)],
                side_send.at[z], side_recv.at[z], dp=beside,
            ).wait()
            return carry

        lax.fori_loop(0, lines, side, 0)
        kept.wait()


def exchange(ids, embedded, gain, proj_grad, weight, stream, n, n_mp, cap, keep, spill, block_rows):
    tokens, width = embedded.shape
    inner = proj_grad.shape[1]
    half = width // 2
    chunk = min(256, half)
    index_width = 3 * LANES if spill else cap
    over = (spill or 16, half)
    kept = (tokens, width) if spill else (8, LANES)
    any_space = pl.BlockSpec(memory_space=pl.ANY)
    vmem = pl.BlockSpec(memory_space=pltpu.VMEM)
    dma = pltpu.SemaphoreType.DMA
    return pl.pallas_call(
        functools.partial(exchange_kernel, n, cap, keep, spill, block_rows, width * n_mp, chunk),
        out_shape=(
            jax.ShapeDtypeStruct((n, 2, keep, half), jnp.bfloat16),
            jax.ShapeDtypeStruct((n, 2, 1, index_width), jnp.int32),
            jax.ShapeDtypeStruct((n if spill else 1, 2) + over, jnp.bfloat16),
            jax.ShapeDtypeStruct(kept, jnp.bfloat16),
        ),
        in_specs=[vmem, vmem] + [any_space] * 4,
        out_specs=(any_space,) * 4,
        scratch_shapes=[
            pltpu.VMEM((tokens, width), jnp.bfloat16),
            pltpu.VMEM((tokens, inner), jnp.bfloat16),
            pltpu.VMEM((width, inner), jnp.bfloat16),
            pltpu.VMEM((tokens, width), jnp.bfloat16),
            pltpu.VMEM((tokens, width), jnp.float32),
            pltpu.VMEM((tokens, width), jnp.bfloat16),
            pltpu.VMEM((n, 2, keep, half), jnp.bfloat16),
            pltpu.VMEM((n, 1, index_width), jnp.int32),
            pltpu.VMEM((2,) + over, jnp.bfloat16),
            pltpu.VMEM((8, tokens), jnp.float32),
            pltpu.VMEM((8, tokens), jnp.float32),
            pltpu.VMEM((n * keep + (LANES if spill else 0), tokens), jnp.bfloat16),
            pltpu.VMEM((8, tokens), jnp.bfloat16),
            pltpu.VMEM((8, LANES), jnp.int32),
            dma((3,)),
            dma((width // chunk,)),
            dma,
            dma,
            dma((n, 2)),
            dma((n, 2)),
            dma((n, 2)),
            dma((n, 2)),
            dma((4,)),
            dma,
            dma,
            dma((2, n)),
            dma((2, n)),
            dma((n,)),
            dma((n,)),
        ],
        compiler_params=pltpu.CompilerParams(
            collective_id=0, has_side_effects=True, vmem_limit_bytes=VMEM_LIMIT
        ),
    )(ids, gain, embedded, proj_grad, weight, stream)


def full_kernel(
    n, cap, block_rows, ids_ref, rows_v, rows_out, index_out, send_v, sendi_v, placer_v, local_v,
    send_sem, recv_sem, isend_sem, irecv_sem, own_sem,
):
    pipe = lax.axis_index("pipe")
    me = lax.axis_index("dp")
    other = 1 - pipe
    barrier = greet_all(n, pipe, other, me, None)
    pl.semaphore_wait(barrier, 2 * n - 1)
    find_places(n, cap, 0, block_rows, me, ids_ref, placer_v, local_v, None)
    place_indices(n, cap, 0, me, placer_v, local_v, None, sendi_v)
    width = rows_v.shape[1]
    chunk = min(256, width // 2)
    for c in range(width // chunk):
        place_rows(c, chunk, cap, 0, placer_v, rows_v[:, c * chunk:(c + 1) * chunk], send_v, None)
    send, arrive = make_sender(
        n, pipe, other, me, send_v, sendi_v, rows_out, index_out,
        (send_sem, recv_sem, isend_sem, irecv_sem),
    )

    def send_on(k, carry):
        send(k, False)
        return carry

    lax.fori_loop(1, n, send_on, 0)
    send(0, True)
    own_rows = pltpu.make_async_copy(send_v.at[0, pipe], rows_out.at[0, pipe], own_sem.at[0])
    own_index = pltpu.make_async_copy(sendi_v.at[0], index_out.at[0, pipe], own_sem.at[1])
    own_rows.start()
    own_index.start()
    lax.fori_loop(0, n, arrive, 0)
    own_rows.wait()
    own_index.wait()


def full_exchange(ids, rows, n, cap, block_rows):
    tokens, width = rows.shape
    half = width // 2
    any_space = pl.BlockSpec(memory_space=pl.ANY)
    vmem = pl.BlockSpec(memory_space=pltpu.VMEM)
    dma = pltpu.SemaphoreType.DMA
    return pl.pallas_call(
        functools.partial(full_kernel, n, cap, block_rows),
        out_shape=(
            jax.ShapeDtypeStruct((n, 2, cap, half), jnp.bfloat16),
            jax.ShapeDtypeStruct((n, 2, 1, cap), jnp.int32),
        ),
        in_specs=[vmem, vmem],
        out_specs=(any_space, any_space),
        scratch_shapes=[
            pltpu.VMEM((n, 2, cap, half), jnp.bfloat16),
            pltpu.VMEM((n, 1, cap), jnp.int32),
            pltpu.VMEM((n * cap, tokens), jnp.bfloat16),
            pltpu.VMEM((8, tokens), jnp.bfloat16),
            dma((n, 2)),
            dma((n, 2)),
            dma((n, 2)),
            dma((n, 2)),
            dma((2,)),
        ],
        compiler_params=pltpu.CompilerParams(
            collective_id=1, has_side_effects=True, vmem_limit_bytes=VMEM_LIMIT
        ),
    )(ids, rows)


def table_kernel(spilled, index_ref, rows_ref, *rest):
    if spilled:
        over_ref, out_ref, wide_v = rest
    else:
        out_ref, wide_v = rest
    blocks, cap, half = rows_ref.shape
    lines = half // LANES
    pieces = 16
    while out_ref.shape[0] % (8 * pieces):
        pieces //= 2
    zero_rows = out_ref.shape[0] // pieces

    def clear(i, carry):
        out_ref[pl.ds(pl.multiple_of(i * zero_rows, 8), zero_rows), :] = jnp.zeros(
            (zero_rows, LANES), jnp.float32
        )
        return carry

    lax.fori_loop(0, pieces, clear, 0)

    def add_row(v, c):
        v = pl.multiple_of(v * lines, lines)
        out_ref[pl.ds(v, lines), :] += wide_v[pl.ds(pl.multiple_of(c * lines, lines), lines), :]

    def block(b, carry):
        for j in range(lines):
            wide_v[pl.ds(j, cap, stride=lines), :] = rows_ref[b, :, j * LANES:(j + 1) * LANES].astype(
                jnp.float32
            )

        def add(g, carry):
            for u in range(8):
                add_row(index_ref[b, 0, g * 8 + u], g * 8 + u)
            return carry

        lax.fori_loop(0, cap // 8, add, 0)
        if spilled:

            @pl.when(index_ref[b, 0, 2 * LANES + 1] > 0)
            def _():
                for j in range(lines):
                    wide_v[pl.ds(j, spilled, stride=lines), :] = over_ref[
                        b, :, j * LANES:(j + 1) * LANES
                    ].astype(
                        jnp.float32
                    )

                count = index_ref[b, 0, 2 * LANES + 1]
                start = index_ref[b, 0, 2 * LANES + 2]

                def add_spilled(g, carry):
                    for u in range(8):
                        here = g * 8 + u < count
                        c = jnp.minimum(start + g * 8 + u, spilled - 1)
                        v = pl.multiple_of(jnp.where(here, index_ref[b, 0, LANES + c], 0) * lines, lines)
                        row = wide_v[pl.ds(pl.multiple_of(c * lines, lines), lines), :]
                        out_ref[pl.ds(v, lines), :] += jnp.where(here, row, 0.0)
                    return carry

                lax.fori_loop(0, (count + 7) // 8, add_spilled, 0)

        return carry

    lax.fori_loop(0, blocks, block, 0)


def table(index, rows, over, block_rows):
    n, stacks, cap, half = rows.shape
    lines = half // LANES
    spilled = 0 if over is None else over.shape[2]
    operands = [index.reshape(n * stacks, 1, -1), rows.reshape(n * stacks, cap, half)]
    in_specs = [pl.BlockSpec(memory_space=pltpu.SMEM), pl.BlockSpec(memory_space=pltpu.VMEM)]
    scratch = [pltpu.VMEM((max(cap, spilled) * lines, LANES), jnp.float32)]
    if spilled:
        operands.append(over.reshape(n * stacks, spilled, half))
        in_specs.append(pl.BlockSpec(memory_space=pltpu.VMEM))
    return pl.pallas_call(
        functools.partial(table_kernel, spilled),
        out_shape=jax.ShapeDtypeStruct((block_rows * lines, LANES), jnp.float32),
        in_specs=in_specs,
        out_specs=pl.BlockSpec(memory_space=pltpu.VMEM),
        scratch_shapes=scratch,
        compiler_params=pltpu.CompilerParams(vmem_limit_bytes=VMEM_LIMIT),
    )(*operands)


def on_device(token_ids, embedded, norm_gain, proj_grad, proj_weight, stream_grad):
    n = lax.axis_size("dp")
    tokens = token_ids.shape[1]
    cap = max(2, 2 * tokens // n)
    block_rows = VOCAB // n
    tiers = cap % 32 == 0 and cap <= LANES
    keep = cap // 2 if tiers else cap
    spill = keep + 16 if tiers else 0
    rows, index, over, kept = exchange(
        token_ids, embedded[0], norm_gain, proj_grad[0], proj_weight[0], stream_grad[0],
        n, lax.axis_size("mp"), cap, keep, spill, block_rows,
    )
    half = rows.shape[-1]
    if tiers:

        def whole():
            full_rows, full_index = full_exchange(token_ids, kept, n, cap, block_rows)
            return table(full_index, full_rows, None, block_rows)

        def short():
            return table(index, rows, over, block_rows)

        out = lax.cond(jnp.max(index[:, :, 0, 2 * LANES]) > 0, whole, short)
    else:
        out = table(index, rows, None, block_rows)
    return out.reshape(block_rows, 1, half)


def solution(mesh):
    return jax.shard_map(
        on_device,
        mesh=mesh,
        in_specs=(
            P("pipe", "dp"),
            P("pipe", "dp", "mp"),
            P("pipe", "mp"),
            P("pipe", "dp", None),
            P("pipe", "mp", None),
            P("pipe", "dp", "mp"),
        ),
        out_specs=P("dp", "mp", "pipe"),
        check_vma=False,
    )
```

profile of v0, /device:TPU:0, one launch (start us, length us, event | category | flops | bytes accessed | tf_op | source)
XLA Modules:
  0.0 107.5 jit_solution(17901963550149285006)
XLA Ops:
  0.0 0.0 copy-start
  0.0 91.8 %shard_map.66 = (bf16[8,2,64,1024]{3,2,1,0:T(8,128)(2,1)}, s32[8,2,1,384]{3,2,1,0:T(1,128)S(1)}, bf16[8,2,80,1024]{3,2,1,0:T(8,128)(2,1)S(1)}, bf16[512,2048]{1,0:T(8,128)(2,1)}) custom-call(s32[1,512]{1,0:T(1,128)} %ids_ref.1, f32[1,2048]{1,0:T(1,128)} %gain_ref.1, bf16[512,2048]{1,0:T(8,128)(2,1)} %bitcast.16, bf16[512,2048]{1,0:T(8,128)(2,1)} %bitcast.17, ...), custom_call_target="tpu_custom_call" | custom-call | tf_op jit(solution)/shard_map/pallas_call | solution.py:348
  91.9 0.6 slice_reduce_fusion
  93.2 0.0 copy-done
  93.2 14.3 %conditional.1 = (f32[4016,1,1024]{2,1,0:T(1,128)}) conditional(s32[]{:T(128)} %convert_element_type.3, (s32[8,2,1,384]{3,2,1,0:T(1,128)S(1)}, bf16[8,2,64,1024]{3,2,1,0:T(8,128)(2,1)}, bf16[8,2,80,1024]{3,2,1,0:T(8,128)(2,1)S(1)}) %tuple.13, (s32[1,512]{1,0:T(1,128)S(1)}, bf16[512,2048]{1,0:T(8,128)(2,1)}) %tuple.21), branch_computations={%region_1.0_spmd, %region_2.0_spmd} | conditional | bytes 8 | solution.py:569
  93.2 14.3 %branch_0_fun.1 = f32[32128,128]{1,0:T(8,128)} custom-call(s32[16,1,384]{2,1,0:T(1,128)S(1)} %bitcast.20, bf16[16,64,1024]{2,1,0:T(8,128)(2,1)} %bitcast.19, bf16[16,80,1024]{2,1,0:T(8,128)(2,1)S(1)} %bitcast.15), custom_call_target="tpu_custom_call" | custom-call | tf_op jit(solution)/shard_map/cond/branch_0_fun/pallas_call | solution.py:537
Async XLA Ops:
  0.0 93.2 %copy-start = (s32[1,512]{1,0:T(1,128)S(1)}, s32[1,512]{1,0:T(1,128)}, u32[]{:S(2)}) copy-start(s32[1,512]{1,0:T(1,128)} %ids_ref.1) | copy-start | bytes 6148
where the time goes:
time: 108 us; the launch traced here: 107 us
  Pallas kernels  106 us (98%)
    pallas_call x1, Pallas kernels, exchange(): pl.pallas_call(functools.partial(exchange_kernel, n, cap, keep, spill, bl...  91.8 us
    pallas_call x1, Pallas kernels, table(): pl.pallas_call(functools.partial(table_kernel, spilled), out_shape=jax.Sh...  14.3 us

commit v1 on v0

--- a/solution.py
+++ b/solution.py
@@ -299,10 +299,11 @@
         own_over.wait()
         pair.wait()
         pass_on(0)
-        for k in range(2, n):
+        for k in range(2, n, 2):
             send(k, False)
-            if k % 2 == 1 and k // 2 < lines:
-                pass_on(k // 2)
+            pass_on(k // 2)
+        for k in range(3, n, 2):
+            send(k, False)
         send(0, True)
     else:
 

time: 108 us -> 113 us (1.046); the launches traced: 107 us -> 115 us
  Pallas kernels: 106 us -> 113 us
    pallas_call x1, Pallas kernels: 91.8 us -> 95.7 us  [exchange(): pl.pallas_call(functools.partial(exchange_kernel, n, cap, keep, spill, bl...]
    pallas_call x1, Pallas kernels: 14.3 us -> 17.6 us  [table(): pl.pallas_call(functools.partial(table_kernel, spilled), out_shape=jax.Sh...]
where the time goes in v1:
time: 113 us; the launch traced here: 115 us
  Pallas kernels  113 us (100%)
    pallas_call x1, Pallas kernels, exchange(): pl.pallas_call(functools.partial(exchange_kernel, n, cap, keep, spill, bl...  95.7 us
    pallas_call x1, Pallas kernels, table(): pl.pallas_call(functools.partial(table_kernel, spilled), out_shape=jax.Sh...  17.6 us

profile of v1, /device:TPU:0, one launch (start us, length us, event | category | flops | bytes accessed | tf_op | source)
XLA Modules:
  0.0 114.6 jit_solution(18403708124223334181)
XLA Ops:
  0.0 0.0 copy-start
  0.0 95.7 %shard_map.66 = (bf16[8,2,64,1024]{3,2,1,0:T(8,128)(2,1)}, s32[8,2,1,384]{3,2,1,0:T(1,128)S(1)}, bf16[8,2,80,1024]{3,2,1,0:T(8,128)(2,1)S(1)}, bf16[512,2048]{1,0:T(8,128)(2,1)}) custom-call(s32[1,512]{1,0:T(1,128)} %ids_ref.1, f32[1,2048]{1,0:T(1,128)} %gain_ref.1, bf16[512,2048]{1,0:T(8,128)(2,1)} %bitcast.16, bf16[512,2048]{1,0:T(8,128)(2,1)} %bitcast.17, ...), custom_call_target="tpu_custom_call" | custom-call | tf_op jit(solution)/shard_map/pallas_call | solution.py:349
  95.7 0.6 slice_reduce_fusion
  97.0 0.0 copy-done
  97.0 17.6 %conditional.1 = (f32[4016,1,1024]{2,1,0:T(1,128)}) conditional(s32[]{:T(128)} %convert_element_type.3, (s32[8,2,1,384]{3,2,1,0:T(1,128)S(1)}, bf16[8,2,64,1024]{3,2,1,0:T(8,128)(2,1)}, bf16[8,2,80,1024]{3,2,1,0:T(8,128)(2,1)S(1)}) %tuple.13, (s32[1,512]{1,0:T(1,128)S(1)}, bf16[512,2048]{1,0:T(8,128)(2,1)}) %tuple.21), branch_computations={%region_1.0_spmd, %region_2.0_spmd} | conditional | bytes 8 | solution.py:570
  97.0 17.6 %branch_0_fun.1 = f32[32128,128]{1,0:T(8,128)} custom-call(s32[16,1,384]{2,1,0:T(1,128)S(1)} %bitcast.20, bf16[16,64,1024]{2,1,0:T(8,128)(2,1)} %bitcast.19, bf16[16,80,1024]{2,1,0:T(8,128)(2,1)S(1)} %bitcast.15), custom_call_target="tpu_custom_call" | custom-call | tf_op jit(solution)/shard_map/cond/branch_0_fun/pallas_call | solution.py:538
Async XLA Ops:
  0.0 97.0 %copy-start = (s32[1,512]{1,0:T(1,128)S(1)}, s32[1,512]{1,0:T(1,128)}, u32[]{:S(2)}) copy-start(s32[1,512]{1,0:T(1,128)} %ids_ref.1) | copy-start | bytes 6148
